TPU v7x, 32 devices: a 4x4x1 block of a 4x4x8 slice. The times are simulated.
32 devices in a mesh: data: 1 (over z), seq: 32 (over y, x, core).
Axes of the slice: x: 4, y: 4, z: 1, core: 2. Of those that a mesh axis runs over, the one named last changes fastest.
The devices are a block of a 4x4x8 slice.
Arguments:
- hidden: bfloat16 [3, 12288, 768], P('data', 'seq')
- positions: int32 [3, 12288], P('data', 'seq')
- g_attn: float32 [1, 768], replicated
- g_mlp: float32 [1, 768], replicated
- w_query: bfloat16 [1, 768, 12, 64], replicated
- w_key: bfloat16 [1, 768, 12, 64], replicated
- w_value: bfloat16 [1, 768, 12, 64], replicated
- w_out: bfloat16 [1, 768, 768], replicated
- w_gate: bfloat16 [1, 768, 3072], replicated
- w_up: bfloat16 [1, 768, 3072], replicated
- w_down: bfloat16 [1, 3072, 768], replicated
- d_out: bfloat16 [3, 12288, 768], P('data', 'seq')
Outputs:
- output 1: bfloat16 [3, 12288, 768], P('data', 'seq')
- output 2: float32 [1, 768], P(None, ('data', 'seq'))
- output 3: float32 [1, 768], P(None, ('data', 'seq'))
- output 4: float32 [1, 768, 12, 64], P(None, ('data', 'seq'))
- output 5: float32 [1, 768, 12, 64], P(None, ('data', 'seq'))
- output 6: float32 [1, 768, 12, 64], P(None, ('data', 'seq'))
- output 7: float32 [1, 768, 768], P(None, ('data', 'seq'))
- output 8: float32 [1, 768, 3072], P(None, ('data', 'seq'))
- output 9: float32 [1, 768, 3072], P(None, ('data', 'seq'))
- output 10: float32 [1, 3072, 768], P(None, ('data', 'seq'))
All inputs are finite; a program needn't handle non-finite values.
Results may differ from a plain program's by a relative error of at most 0.02.
Values are sent between devices in bfloat16 or wider.
A program may use at most 768 MiB of HBM per device.

v0:
```python
import functools, math
import numpy as np
import jax, jax.numpy as jnp
from jax import lax
from jax.experimental import pallas as pl
from jax.experimental.pallas import tpu as pltpu
from jax.sharding import PartitionSpec as P

WINDOW = 256
NORM_EPS = 1e-5
QB = 128
BF, F32 = jnp.bfloat16, jnp.float32
NN, NT, TN = ((1,), (0,)), ((1,), (1,)), ((0,), (0,))
MESH = pl.DeviceIdType.MESH
NEG = -1e30
VMEM_LIMIT = 67043328


def dot(a, b, dims=NN):
    return lax.dot_general(a, b, (dims, ((), ())), preferred_element_type=F32)


def cdiv_loop(n, body):
    lax.fori_loop(0, n, lambda i, c: body(i) or c, 0)


def mod(a, b):
    return a % b if isinstance(a, int) else lax.rem(a, b)


def aligned(a, b):
    return a if isinstance(a, int) else pl.multiple_of(a, b)


def rope(blk, cos_b, sin_b, sign, head_dim):
    half = head_dim // 2
    parts = []
    for h in range(blk.shape[0] // head_dim):
        first = blk[h * head_dim:h * head_dim + half]
        second = blk[h * head_dim + half:(h + 1) * head_dim]
        if sign > 0:
            parts += [first * cos_b - second * sin_b, second * cos_b + first * sin_b]
        else:
            parts += [first * cos_b + second * sin_b, second * cos_b - first * sin_b]
    return jnp.concatenate(parts, axis=0)


def normed(x, gain):
    xf = x.astype(F32)
    inv = lax.rsqrt(jnp.mean(xf * xf, axis=-1, keepdims=True) + NORM_EPS)
    return (xf * inv * gain).astype(BF)


def stack_pair(pair_t):
    half = pair_t.shape[0] // 2
    zero = jnp.zeros((half, pair_t.shape[1]), pair_t.dtype)
    return jnp.concatenate(
        [jnp.concatenate([pair_t[:half], zero], axis=0), jnp.concatenate([zero, pair_t[half:]], axis=0)], axis=1)


def unstack_pair(both):
    half, cols = both.shape[0] // 2, both.shape[1] // 2
    return jnp.concatenate([both[:half, :cols], both[half:, cols:]], axis=0)


def col_sum(x):
    return jnp.sum(x, axis=0, keepdims=True)


def merged(scores, upper, bias0, bias1):
    return jnp.where(upper, scores[:QB] + bias0, scores[2 * QB:]), scores[QB:2 * QB] + bias1


def banded(p02, p1, upper):
    return jnp.concatenate(
        [jnp.where(upper, p02, 0.0).astype(BF), p1.astype(BF), jnp.where(upper, 0.0, p02).astype(BF)], axis=0)


def upper_mask():
    key_ids = lax.broadcasted_iota(jnp.int32, (QB, 2 * QB), 0)
    query_ids = lax.broadcasted_iota(jnp.int32, (QB, 2 * QB), 1) % QB
    return key_ids > query_ids


def start_bias(first, blk):
    bias = jnp.where(first, NEG, 0.0).astype(F32)
    return (bias if blk < 2 else 0.0), (bias if blk < 1 else 0.0)


def fwd_kernel(n, head_dim, x_h, pos_h, invf_h, ga_h, gm_h, wq_h, wk_h, wv_h, wo_h,
               q_h, kt_h, k_h, v_h, ha_h, ot_h, xm_h, hm_h, hmt_h, qr_h, lse_h, cos_t, sin_t,
               pos, invf, ga, gm, xv, halo, qr, lse, pos_halo, wq, wk, wv, wo, q, kt, k, v, vt, ot, xm, hm, hmt, hb, hh, acc, acc2, ak, av, cos_h, sin_h,
               sc0, sc1, sc2, pb0, pb1, pb2, ldx, ld, st, snd, rcv, qsnd, qrcv):
    sc, pb = (sc0, sc1, sc2), (pb0, pb1, pb2)
    rows, toks, width = xv.shape
    ext, total, pw = toks + WINDOW, rows * toks, 2 * head_dim
    n_pairs = wq.shape[0] // pw
    tb, n_steps = toks // QB, n_pairs * rows
    me = lax.axis_index("seq")
    right, left = lax.rem(me + 1, n), lax.rem(me + n - 1, n)
    load_x = [pltpu.make_async_copy(x_h.at[b], xv.at[b], ldx.at[b]) for b in range(rows)]
    load_w = [pltpu.make_async_copy(s, d, ld.at[i]) for i, (s, d) in enumerate(((wq_h, wq), (wk_h, wk), (wv_h, wv), (wo_h, wo)))]
    load_s = [pltpu.make_async_copy(s, d, ldx.at[rows + i]) for i, (s, d) in enumerate(((pos_h, pos), (invf_h, invf), (ga_h, ga), (gm_h, gm)))]
    for c in load_s + load_x:
        c.start()
    barrier = pltpu.get_barrier_semaphore()
    for other in (left, right):
        pl.semaphore_signal(barrier, inc=1, device_id={"seq": other}, device_id_type=MESH)

    def push(i, s, d):
        return pltpu.make_async_remote_copy(src_ref=s, dst_ref=d, send_sem=snd.at[i], recv_sem=rcv.at[i], device_id={"seq": right}, device_id_type=MESH)

    def push_rows(b):
        return push(b, x_h.at[b, toks - WINDOW:, :], halo.at[b])

    send_pos = push(rows, pos, pos_halo)

    def angles(cos_ref, sin_ref, positions):
        count = positions.shape[1]
        for b in range(rows):
            ang = invf[:] * positions[b:b + 1, :].astype(F32)
            cos_ref[:, b * count:(b + 1) * count] = jnp.cos(ang)
            sin_ref[:, b * count:(b + 1) * count] = jnp.sin(ang)

    for c in load_s:
        c.wait()
    angles(cos_t, sin_t, pos[:])

    def norm_rows(b):
        for i in range(tb):
            h = normed(xv[b, i * QB:(i + 1) * QB, :], ga[:])
            hb[pl.ds(pl.multiple_of((b * tb + i) * QB, QB), QB), :] = h

    with jax.named_scope("f_norm"):
        for c in load_x:
            c.wait()
        for c in load_w:
            c.start()
        cdiv_loop(rows, norm_rows)
    pl.semaphore_wait(barrier, 2)
    send_pos.start()
    for b in range(rows):
        push_rows(b).start()
    keep_ha = pltpu.make_async_copy(hb, ha_h, st.at[0])
    keep_ha.start()
    tables = cos_t[:], sin_t[:]

    def put_q(src):
        for p in range(n_pairs):
            r = slice(p * pw, (p + 1) * pw)
            q[r, :] = (rope(src[r, :], *tables, 1, head_dim) * (head_dim ** -0.5)).astype(BF)

    def put_own(src, dst_t, dst):
        for p in range(n_pairs):
            r = slice(p * pw, (p + 1) * pw)
            both = (rope(src[r, :], *tables, 1, head_dim) if dst is k else src[r, :]).astype(BF)
            for b in range(rows):
                blk = both[:, b * toks:(b + 1) * toks]
                own = slice(b * ext + WINDOW, (b + 1) * ext)
                dst_t[r, own] = blk
                dst[own, r] = blk.T

    with jax.named_scope("f_mm"):
        load_w[0].wait()
        load_w[1].wait()
        load_w[2].wait()
        acc[:] = dot(wq[:], hb[:], NT)
        acc2[:] = dot(wk[:], hb[:], NT)
        put_q(acc)
        acc[:] = dot(wv[:], hb[:], NT)
        put_own(acc2, kt, k)
        put_own(acc, vt, v)
    keep_q = pltpu.make_async_copy(q, q_h, st.at[1])
    keep_q.start()

    def push_q(b):
        return pltpu.make_async_remote_copy(src_ref=q.at[:, b * toks:b * toks + WINDOW], dst_ref=qr.at[:, b * WINDOW:(b + 1) * WINDOW],
                                            send_sem=qsnd.at[b], recv_sem=qrcv.at[b], device_id={"seq": left}, device_id_type=MESH)

    for b in range(rows):
        push_q(b).start()
    send_pos.wait()
    angles(cos_h, sin_h, pos_halo[:, toks - WINDOW:])

    def keeps(b):
        wide, cols = pl.ds(pl.multiple_of(b * ext, QB), ext), pl.ds(pl.multiple_of(b * toks, QB), toks)
        ends = ((kt.at[:, wide], kt_h.at[:, wide]), (k.at[wide, :], k_h.at[wide, :]), (v.at[wide, :], v_h.at[wide, :]),
                (ot.at[:, cols], ot_h.at[:, cols]), (hm.at[cols, :], hm_h.at[cols, :]), (hmt.at[:, cols], hmt_h.at[:, cols]),
                (xm.at[cols, :], xm_h.at[cols, :]))
        return [pltpu.make_async_copy(s, d, st.at[2 + b * len(ends) + i]) for i, (s, d) in enumerate(ends)]

    def halo_in(b):
        with jax.named_scope("f_halo_wait"):
            push_rows(b).wait()
        with jax.named_scope("f_halo"):
            for i in range(WINDOW // QB):
                r = slice(i * QB, (i + 1) * QB)
                hh[r, :] = normed(halo[b, r, :], ga[:])
            ak[:] = dot(wk[:], hh[:], NT)
            av[:] = dot(wv[:], hh[:], NT)
            cols = pl.ds(pl.multiple_of(b * WINDOW, QB), WINDOW)
            wide = pl.ds(pl.multiple_of(b * ext, QB), WINDOW)
            near = cos_h[:, cols], sin_h[:, cols]
            for src, dst_t, dst in ((ak, kt, k), (av, vt, v)):
                for p in range(n_pairs):
                    r = slice(p * pw, (p + 1) * pw)
                    blk = (rope(src[r, :], *near, 1, head_dim) if dst is k else src[r, :]).astype(BF)
                    dst_t[r, wide] = blk
                    dst[wide, r] = blk.T
        for c in keeps(b)[:3]:
            c.start()

    upper = upper_mask()
    first = me == 0

    def spots(it, blk):
        b, p = it // n_pairs, mod(it, n_pairs)
        pr = pl.ds(aligned(p * pw, pw), pw)
        return pr, pl.ds(aligned(b * toks + blk * QB, QB), QB), pl.ds(aligned(b * ext + blk * QB, QB), 3 * QB)

    def score(it):
        for blk in range(tb):
            pr, cols, keys = spots(it, blk)
            sc[blk][:] = dot(k[keys, pr], stack_pair(q[pr, cols]))

    def soften(it, blk):
        s02, s1 = merged(sc[blk][:], upper, *start_bias(first, blk))
        top = jnp.max(jnp.maximum(s02, s1), axis=0, keepdims=True)
        e02, e1 = jnp.exp(s02 - top), jnp.exp(s1 - top)
        mass = col_sum(e02 + e1)
        inv = 1.0 / mass
        lse[it, blk:blk + 1, :] = top + jnp.log(mass)
        pb[blk][:] = banded(e02 * inv, e1 * inv, upper)

    def mix(it):
        for blk in range(tb):
            pr, cols, keys = spots(it, blk)
            ot[pr, cols] = unstack_pair(dot(vt[pr, keys], pb[blk][:])).astype(BF)

    def project(b):
        cols = pl.ds(pl.multiple_of(b * toks, QB), toks)
        with jax.named_scope("f_proj"):
            mid = (xv[b].astype(F32) + dot(ot[:, cols], wo[:], TN)).astype(BF)
            xm[cols, :] = mid
            h = normed(mid, gm[:])
            hm[cols, :] = h
            hmt[:, cols] = h.T
        for c in keeps(b)[3:]:
            c.start()

    keep_qr, keep_lse = (pltpu.make_async_copy(*ends, ld.at[i]) for i, ends in enumerate(((qr, qr_h), (lse, lse_h))))
    load_w[3].wait()
    for blk in range(tb):
        pb[blk][:] = jnp.zeros(pb[blk].shape, BF)

    def walk(i):
        it = i - 1

        @pl.when((lax.rem(i, n_pairs) == 0) & (i < n_steps))
        def _():
            halo_in(i // n_pairs)

        @pl.when(i == 0)
        def _():
            score(0)

        @pl.when((i > 0) & (i <= n_steps))
        def _():
            with jax.named_scope("f_attn"):
                mix(jnp.maximum(it - 1, 0))
                for blk in range(tb):
                    soften(it, blk)
                score(jnp.minimum(i, n_steps - 1))

        @pl.when(i == n_steps)
        def _():
            for b in range(rows):
                push_q(b).wait()
            keep_qr.start()

        @pl.when(i > n_steps)
        def _():
            mix(n_steps - 1)

        @pl.when((lax.rem(it, n_pairs) == 0) & (it > 0))
        def _():
            project(it // n_pairs - 1)

    cdiv_loop(n_steps + 2, walk)
    with jax.named_scope("f_store_wait"):
        keep_lse.start()
        keep_ha.wait()
        keep_q.wait()
        keep_qr.wait()
        keep_lse.wait()
        for b in range(rows):
            for c in keeps(b):
                c.wait()


def any_spec(k):
    return [pl.BlockSpec(memory_space=pl.ANY)] * k


def vmem_spec(k):
    return [pl.BlockSpec(memory_space=pltpu.VMEM)] * k


def run_fwd(n, x, pos, invf, ga, gm, wq, wk, wv, wo, head_dim):
    rows, toks, width = x.shape
    hd = wq.shape[0]
    ext, total, n_halo = toks + WINDOW, rows * toks, rows * WINDOW
    half = head_dim // 2
    sds = lambda *s: jax.ShapeDtypeStruct(s, BF)
    dma = lambda *s: pltpu.SemaphoreType.DMA(s)
    outs = [sds(hd, total), sds(hd, rows * ext), sds(rows * ext, hd), sds(rows * ext, hd), sds(total, width), sds(hd, total), sds(total, width), sds(total, width), sds(width, total)]
    outs += [sds(hd, n_halo), jax.ShapeDtypeStruct((rows * hd // (2 * head_dim), 8, 2 * QB), F32)] + [jax.ShapeDtypeStruct((half, total), F32)] * 2
    vm = lambda *s: pltpu.VMEM(s, BF)
    vf = lambda *s: pltpu.VMEM(s, F32)
    scratch = [pltpu.VMEM((rows, toks), jnp.int32), vf(*invf.shape), vf(*ga.shape), vf(*ga.shape), vm(rows, toks, width), vm(rows, WINDOW, width), vm(hd, n_halo), vf(rows * hd // (2 * head_dim), 8, 2 * QB), pltpu.VMEM((rows, toks), jnp.int32), vm(hd, width), vm(hd, width), vm(hd, width), vm(hd, width),
               vm(hd, total), vm(hd, rows * ext), vm(rows * ext, hd), vm(rows * ext, hd), vm(hd, rows * ext), vm(hd, total), vm(total, width), vm(total, width), vm(width, total), vm(total, width), vm(WINDOW, width),
               vf(hd, total), vf(hd, total), vf(hd, WINDOW), vf(hd, WINDOW), vf(half, n_halo), vf(half, n_halo),
               *[f(3 * QB, 2 * QB) for f in (vf, vm) for _ in range(3)],
               dma(rows + 4), dma(4), dma(2 + 7 * rows), dma(rows + 1), dma(rows + 1), dma(rows), dma(rows)]
    return pl.pallas_call(
        functools.partial(fwd_kernel, n, head_dim), out_shape=outs,
        in_specs=any_spec(9), out_specs=any_spec(11) + vmem_spec(2), scratch_shapes=scratch,
        compiler_params=pltpu.CompilerParams(collective_id=0, has_side_effects=True, vmem_limit_bytes=VMEM_LIMIT),
        name="forward")(x, pos, invf, ga, gm, wq, wk, wv, wo)


LAG = 2
SLOTS = 2 * LAG
RING = 8
CB = 256


def at(ref, *idx):
    return ref.at[idx]


class Torus:
    def __init__(self, n, head, last, turn, parts, recv0, recv1, recv2, recv3, recv4, recv5, acc, acc2, fin, snd, rcv):
        assert math.isqrt(n // 2) == 4
        me = lax.axis_index("seq")
        self.core = lax.rem(me, 2)
        chip = me // 2
        self.x, self.y = lax.rem(chip, 4), chip // 4
        self.head, self.last, self.turn = head, last, turn
        self.parts, self.recv0, self.recv1, self.recv2, self.recv3, self.recv4, self.recv5 = parts, recv0, recv1, recv2, recv3, recv4, recv5
        self.acc, self.acc2, self.fin, self.snd, self.rcv = acc, acc2, fin, snd, rcv
        self.partner = me + 1 - 2 * self.core
        self.rows, self.columns = [lax.rem(self.y + d, 4) * 4 for d in range(4)], [lax.rem(self.x + d, 4) for d in range(4)]
        self.hops = [[self.device(0, d) for d in range(4)], [self.device(d, 0) for d in range(4)]]

    def device(self, dy, dx):
        return (self.rows[dy] + self.columns[dx]) * 2 + self.core

    def copy(self, lane, kind, slot, src, dst, target):
        return pltpu.make_async_remote_copy(
            src_ref=src, dst_ref=dst, send_sem=self.snd.at[lane, kind, slot], recv_sem=self.rcv.at[lane, kind, slot],
            device_id={"seq": target}, device_id_type=MESH)

    def late(self, axis, pair, yes, no):
        first, end = self.turn
        busy = (pair >= first) & (pair < end)
        return jnp.where(busy & (self.x == 3) if axis else busy, yes, no)

    def swap(self, ring, slot):
        return self.copy(0, 0, slot, self.parts.at[ring, :, :, 1 - self.core], self.recv0.at[slot], self.partner)

    def landing(self, stage):
        return (self.recv0, self.recv1, self.recv2, self.recv3, self.recv4, self.recv5)[stage]

    def arrived(self, stage, kind, slot):
        whole = self.landing(stage).at[kind, slot]
        self.copy(stage, kind, slot, whole, whole, self.partner).wait()

    def send(self, stage, kind, pair, held, slot):
        axis = kind if stage < 3 else 1 - kind
        plus, minus = self.hops[axis][1], self.hops[axis][-1]
        half = CB // 2
        if stage == 1:
            minus = self.late(axis, pair, plus, minus)
            ends = self.acc.at[kind, held, 2, :2], self.acc.at[kind, held, 2, 2:]
        elif stage == 2:
            ends = self.acc.at[kind, held, 1], self.acc.at[kind, held, 3]
        elif stage == 3:
            ends = self.acc2.at[kind, held, 2, :, :half], self.acc2.at[kind, held, 2, :, half:]
        else:
            ends = self.acc2.at[kind, held, 1], self.acc2.at[kind, held, 3]
        for i, src in enumerate(ends):
            self.copy(stage, kind, slot, src, self.landing(stage).at[kind, slot, i], (plus, minus)[i]).start()

    def add(self, stage, kind, pair, held, slot, ring):
        acc, acc2 = self.acc, self.acc2
        if stage == 1:
            for r1 in range(4):
                for r2 in range(4):
                    ry, rx = (r2, r1) if kind == 0 else (r1, r2)
                    chip = self.rows[ry] + self.columns[rx]
                    acc[kind, held, r1, r2] = self.parts[ring, kind, chip, self.core] + self.recv0[slot, kind, chip]
        elif stage == 2:
            back = self.late(kind, pair, 1, 3)
            acc[kind, held, 1, :2] += self.recv1[kind, slot, 0]
            acc[kind, held, back, 2:] += self.recv1[kind, slot, 1]
        elif stage == 3:
            acc2[kind, held] = acc[kind, held, 0] + (self.recv2[kind, slot, 0] + self.recv2[kind, slot, 1])
        elif stage == 4:
            half = CB // 2
            acc2[kind, held, 1, :, :half] += self.recv3[kind, slot, 0]
            acc2[kind, held, 3, :, half:] += self.recv3[kind, slot, 1]
        else:
            self.fin[pair, kind] = acc2[kind, held, 0] + (self.recv4[kind, slot, 0] + self.recv4[kind, slot, 1])

    def direct(self, kind, held, slot):
        for d in range(1, 4):
            self.copy(5, kind, slot, self.acc2.at[kind, held, d], self.recv5.at[kind, slot, d - 1], self.hops[1 - kind][d]).start()

    def early(self, pair):
        return (pair >= 0) & (pair <= self.head)

    def final(self, pair):
        return (pair == self.last) | ((pair > self.head) & (pair < self.last) & (mod(abs(pair - self.head), 2) == 0))

    def when(self, which, fn):
        if isinstance(which, bool):
            fn() if which else None
        else:
            pl.when(which)(fn)

    def offer(self, t):
        self.when(self.early(t) | self.final(t), lambda: self.swap(mod(t, RING), mod(t, SLOTS)).start())

    def tick(self, t):
        self.offer(t)
        self.advance(t)

    def advance(self, t, tail=False):
        now, land, before = mod(t, SLOTS), mod(t + SLOTS - LAG, SLOTS), mod(t + SLOTS - 1, SLOTS)
        ring_land = mod(t + RING - 1, RING)
        for stage in range(5, 0, -1):
            pair = t - LAG * stage + 1
            held = before if stage % 2 else mod(t + 1, SLOTS)

            def move(last_hops, stage=stage, pair=pair, held=held):
                if stage == 1:
                    with jax.named_scope("t_wait1"):
                        self.swap(ring_land, before).wait()
                for kind in range(2):
                    if last_hops and stage == 4:
                        with jax.named_scope("t_wait6"):
                            self.arrived(5, kind, land)
                        got = self.recv5[kind, land]
                        self.fin[pair, kind] = self.acc2[kind, held, 0] + (got[0] + got[1] + got[2])
                        continue
                    if stage > 1:
                        with jax.named_scope(f"t_wait{stage}"):
                            self.arrived(stage - 1, kind, land)
                    self.add(stage, kind, pair, held, land if stage > 1 else before, ring_land)
                    if last_hops and stage == 3:
                        self.direct(kind, held, now)
                    elif stage < 5:
                        self.send(stage, kind, pair, held, now)

            if stage < 3:
                self.when(self.early(pair) | self.final(pair), functools.partial(move, False))
            else:
                self.when(self.early(pair), functools.partial(move, False))
                if tail and stage < 5:
                    self.when(self.final(pair), functools.partial(move, True))


def pick(i, table):
    out = 0
    for key, value in table.items():
        out = jnp.where(i == key, value, out)
    return out


def norm_back(x, gain, grad, res):
    xf = x.astype(F32)
    inv = lax.rsqrt(jnp.mean(xf * xf, axis=-1, keepdims=True) + NORM_EPS)
    unit = xf * inv
    gu = grad * gain
    out = inv * (gu - unit * jnp.mean(gu * unit, axis=-1, keepdims=True)) + res.astype(F32)
    gu = grad * unit
    return out.astype(BF), jnp.sum(gu.reshape(-1, 8, gu.shape[-1]), axis=0)


def plan(n_mlp, n_down, nc):
    order = [("o", g) for g in range(nc)] + [(name, g) for g in range(nc) for name in "qkv"]
    base, head = n_mlp + n_down, n_mlp + n_down + nc - 1
    last = 2 * (base - 1 - head + len(order) // 2) + head - 1
    spot = lambda pair: min(max(pair, 2 * pair - head), last)
    return head, {name: (spot(base + i // 2), i % 2) for i, name in enumerate(order)}, last


def bwd_kernel(n, head_dim, dims, ga_h, gm_h, x_h, dout_h, q_h, kt_h, k_h, v_h, ha_h, ot_h, xm_h, hm_h, hmt_h, qr_h, lse_h, cos_h, sin_h,
               wq_h, wk_h, wv_h, wo_h, wg_h, wu_h, wd_h,
               dx_h, fin_h,
               parts, recv0, recv1, recv2, recv3, recv4, recv5, acc, acc2, fin, snd, rcv,
               dor, lser, deltar, hsnd, hrcv, osnd, orcv, gsend, grecv, gsem, ld,
               xbuf, mbuf, gnm, gmid, ot, hat, wo, dot_, lse, delta, cos_i, sin_i, ga, gm, dgain):
    rows, toks, width, hd, ff = dims
    ext, total = toks + WINDOW, rows * toks
    pw = 2 * head_dim
    n_pairs = hd // pw
    tb, n_steps = toks // QB, n_pairs * rows
    nb, nc, sub = ff // CB, width // CB, ff // width
    rpd = width // n
    per, half_sub = CB // pw, sub // 2
    head, place, end = plan(nb, nc * half_sub, nc)
    comm = Torus(n, head, end, (nb, nb + n_pairs + 1), parts, recv0, recv1, recv2, recv3, recv4, recv5, acc, acc2, fin, snd, rcv)
    me = lax.axis_index("seq")
    left = lax.rem(me + n - 1, n)
    barrier = pltpu.get_barrier_semaphore()

    def greet(i):
        pl.semaphore_signal(barrier, inc=1, device_id={"seq": lax.rem(me + i + 1, n)}, device_id_type=MESH)

    def load(i, s, d):
        c = pltpu.make_async_copy(s, d, ld.at[i])
        c.start()
        return c

    def late(i):
        s, d = ((xm_h, mbuf), (ot_h, ot), (wo_h, wo), (lse_h, lse), (cos_h, cos_i), (sin_h, sin_i), (ga_h, ga), (gm_h, gm))[i]
        return pltpu.make_async_copy(s, d, ld.at[1 + i])

    def to_left(src, dst, send_sem, recv_sem):
        return pltpu.make_async_remote_copy(src_ref=src, dst_ref=dst, send_sem=send_sem, recv_sem=recv_sem,
                                            device_id={"seq": left}, device_id_type=MESH)

    n_late = 8

    def push_rows(i):
        return to_left(*((lse_h, lser), (delta, deltar))[i], hsnd.at[i], hrcv.at[i])

    def push_out(p):
        pr = pl.ds(aligned(p * pw, pw), pw)
        return [to_left(dot_.at[pr, pl.ds(b * toks, WINDOW)], dor.at[pr, pl.ds(b * WINDOW, WINDOW)], osnd.at[p], orcv.at[p])
                for b in range(rows)]

    def give_out(p):
        for c in push_out(p):
            c.start()

    def put(spot, value):
        pair, kind = spot
        parts[mod(pair, RING), kind] = value.reshape(n // 2, 2, rpd, CB)

    def spot_of(name, g):
        known = {i: place[name, i] for i in range(nc)}
        return pick(g, {i: s[0] for i, s in known.items()}), pick(g, {i: s[1] for i, s in known.items()})

    def spots(it, blk):
        p, b = it // rows, mod(it, rows)
        pr = pl.ds(aligned(p * pw, pw), pw)
        return pr, pl.ds(aligned(b * toks + blk * QB, QB), QB), pl.ds(aligned(b * ext + blk * QB, QB), 3 * QB)

    def row_of(it):
        return mod(it, rows) * n_pairs + it // rows

    def mlp(hm, hmt, ha, actt, wgu, wd, dgu, wld):
        def weights(j, slot):
            c = aligned(j * CB, CB)
            return [pltpu.make_async_copy(wg_h.at[:, pl.ds(c, CB)], wgu.at[slot, :, :CB], wld.at[slot, 0]),
                    pltpu.make_async_copy(wu_h.at[:, pl.ds(c, CB)], wgu.at[slot, :, CB:], wld.at[slot, 1]),
                    pltpu.make_async_copy(wd_h.at[pl.ds(c, CB), :], wd.at[slot], wld.at[slot, 2])]

        for c in weights(0, 0):
            c.start()
        ld_hm, ld_x, ld_hmt = load(10, hm_h, hm), load(0, dout_h, xbuf), load(11, hmt_h, hmt)
        cdiv_loop(n - 1, greet)
        gnm[:] = jnp.zeros_like(gnm)
        gsend[:] = jnp.zeros_like(gsend)
        dgain[:] = jnp.zeros_like(dgain)
        ld_hm.wait()
        ld_x.wait()
        ld_hmt.wait()
        for i in range(n_late):
            late(i).start()
        ld_ha = load(10, ha_h, ha)

        def block(j):
            slot = lax.rem(j, 2)
            for c in weights(j, slot):
                c.wait()

            @pl.when(j + 1 < nb)
            def _():
                for c in weights(j + 1, 1 - slot):
                    c.start()

            c0 = pl.multiple_of(j * CB, CB)
            with jax.named_scope("b_mlp"):
                for b in range(rows):
                    r = slice(b * toks, (b + 1) * toks)
                    gu = dot(hm[r, :], wgu[slot])
                    gact = dot(xbuf[r, :], wd[slot], NT).astype(BF).astype(F32)
                    gate, up = gu[:, :CB], gu[:, CB:]
                    sig = 1.0 / (1.0 + jnp.exp(-gate))
                    swish = gate * sig
                    actt[pl.ds(c0, CB), r] = (swish * up).astype(BF).T
                    dgu[r, :CB] = (gact * up * (sig + swish * (1.0 - sig))).astype(BF)
                    dgu[r, CB:] = (gact * swish).astype(BF)
                both = dot(hmt[:], dgu[:])
                ring = lax.rem(j, RING)
                parts[ring, 0] = both[:, :CB].reshape(n // 2, 2, rpd, CB)
                parts[ring, 1] = both[:, CB:].reshape(n // 2, 2, rpd, CB)
                for b in range(rows):
                    r = slice(b * toks, (b + 1) * toks)
                    gnm[r, :] += dot(dgu[r, :], wgu[slot], NT)

            @pl.when(j == 0)
            def _():
                pl.semaphore_wait(barrier, n - 1)
                push_rows(0).start()

            comm.tick(j)

        cdiv_loop(nb, block)

        def down(c):
            share = n // 2 // sub
            c0 = pl.multiple_of(c * CB, CB)
            for m in range(sub):
                res = dot(actt[m * width:(m + 1) * width, :], xbuf[:, pl.ds(c0, CB)]).reshape(share, 2, sub, rpd, CB)
                for i in range(sub):
                    pair = nb + c * half_sub + i // 2
                    parts[lax.rem(pair, RING), i % 2, m * share:(m + 1) * share] = res[:, :, i]
            for i in range(tb * rows // nc):
                r = pl.ds(pl.multiple_of((c * (tb * rows // nc) + i) * QB, QB), QB)
                hat[:, r] = ha[r, :].T

        for i in range(n_late):
            late(i).wait()
        ld_ha.wait()

        def mid(b):
            for i in range(tb):
                r = pl.ds(pl.multiple_of((b * tb + i) * QB, QB), QB)
                out, dg = norm_back(mbuf[r, :], gm[:], gnm[r, :], xbuf[r, :])
                gmid[r, :] = out
                dgain[8:, :] += dg

        def deltas(p):
            for it in range(rows):
                for blk in range(tb):
                    pr, cols, _ = spots(p * rows + it, blk)
                    both = dot_[pr, cols].astype(F32) * ot[pr, cols].astype(F32)
                    delta[row_of(p * rows + it), blk:blk + 1, :] = jnp.concatenate(
                        [col_sum(both[:head_dim]), col_sum(both[head_dim:])], axis=1)

        def column(c):
            with jax.named_scope("b_down"):
                down(c)

            @pl.when(c < nc - 1)
            def _():
                comm.tick(nb + c + jnp.minimum(c, 1))

            @pl.when(c > 0)
            def _():
                give_out(c)

            @pl.when(c == 0)
            def _():
                with jax.named_scope("b_mid"):
                    cdiv_loop(rows, mid)
                with jax.named_scope("b_dot"):
                    dot_[:] = dot(wo[:], gmid[:], NT).astype(BF)
                    cdiv_loop(n_pairs, deltas)
                comm.tick(nb + 1)
                push_rows(1).start()
                give_out(0)

        cdiv_loop(nc, column)

    vm = lambda *s: pltpu.VMEM(s, BF)
    vf = lambda *s: pltpu.VMEM(s, F32)
    pl.run_scoped(mlp, vm(total, width), vm(width, total), vm(total, width), vm(ff, total), vm(2, width, 2 * CB), vm(2, CB, width), vm(total, 2 * CB),
                  pltpu.SemaphoreType.DMA((2, 3)))
    def attention(q, kt, k, v, qr, dv, sc0, sc1, sc2, sr, dp0, dp1, dp2, dr, pb0, pb1, pb2, pr_, ds0, ds1, ds2, dsr):
        dqt, dkt = ot, q
        wq, wk, wv = k.at[:hd], kt.at[:, :width], v.at[:hd]
        sc, dp, pb, ds = (sc0, sc1, sc2), (dp0, dp1, dp2), (pb0, pb1, pb2), (ds0, ds1, ds2)
        lds = [load(10 + i, s, d) for i, (s, d) in enumerate(((q_h, q), (k_h, k), (v_h, v), (qr_h, qr), (kt_h, kt)))]

        def out_grad(g):
            put(spot_of("o", g), dot(ot[:], gmid[:, pl.ds(pl.multiple_of(g * CB, CB), CB)]))

        with jax.named_scope("b_dwo"):
            cdiv_loop(nc, out_grad)
        first_tick = nb + nc + 1
        comm.tick(first_tick - 1)
        ends = [rows * p for p in range(1, n_pairs + 1)]
        steps = sorted([1, ends[1] - 1, ends[-2] - 1, ends[-1] - 1, *ends[1:]])
        tick_after = {s: first_tick + i for i, s in enumerate(steps)}
        assert first_tick + len(steps) == end
        upper = upper_mask()
        first, last = me == 0, me == n - 1
        halves = slice(0, WINDOW), slice(WINDOW, 3 * QB)

        def right(it, i):
            p, b = it // rows, mod(it, rows)
            return pl.ds(aligned(p * pw, pw), pw), pl.ds(aligned(b * WINDOW + i * QB, QB), QB), pl.ds(aligned(b * ext + toks + i * QB, QB), WINDOW - i * QB)

        def score(it):
            for blk in range(tb):
                pr, cols, keys = spots(it, blk)
                sc[blk][:] = dot(k[keys, pr], stack_pair(q[pr, cols]))
                dp[blk][:] = dot(v[keys, pr], stack_pair(dot_[pr, cols]))
            for i, rs in enumerate(halves):
                pr, cols, keys = right(it, i)
                sr[rs, :] = dot(k[keys, pr], stack_pair(qr[pr, cols]))
                dr[rs, :] = dot(v[keys, pr], stack_pair(dor[pr, cols]))

        def soften(it):
            row = row_of(it)
            for blk in range(tb):
                s02, s1 = merged(sc[blk][:], upper, *start_bias(first, blk))
                norm, mean = lse[row, blk:blk + 1, :], delta[row, blk:blk + 1, :]
                p02, p1 = jnp.exp(s02 - norm), jnp.exp(s1 - norm)
                g02, g1 = jnp.where(upper, dp[blk][:QB], dp[blk][2 * QB:]), dp[blk][QB:2 * QB]
                pb[blk][:] = banded(p02, p1, upper)
                ds[blk][:] = banded(p02 * (g02 - mean), p1 * (g1 - mean), upper)
            for blk in range(tb):
                i = blk // 2
                rs = slice(blk * QB, (blk + 1) * QB)
                p = jnp.exp(sr[rs, :] - jnp.where(last, -NEG, lser[row, i:i + 1, :]))
                g = p * (dr[rs, :] - deltar[row, i:i + 1, :])
                pr_[rs, :] = (p if blk == 1 else jnp.where(upper, p, 0.0)).astype(BF)
                dsr[rs, :] = (g if blk == 1 else jnp.where(upper, g, 0.0)).astype(BF)

        def grads(it):
            ks, vs = [], []
            for blk in range(tb):
                pr, cols, keys = spots(it, blk)
                own = slice(max(0, 2 - blk) * QB, 3 * QB)
                vs.append(dot(pb[blk][own, :], stack_pair(dot_[pr, cols]), NT))
                ks.append(dot(ds[blk][own, :], stack_pair(q[pr, cols]), NT))
                dq = unstack_pair(dot(kt[pr, keys], ds[blk][:])) * (head_dim ** -0.5)
                dqt[pr, cols] = rope(dq, cos_i[:, cols], sin_i[:, cols], -1, head_dim).astype(BF)
            for i, rs in enumerate(halves):
                pr, cols, _ = right(it, i)
                vs.append(dot(pr_[rs, :], stack_pair(dor[pr, cols]), NT))
                ks.append(dot(dsr[rs, :], stack_pair(qr[pr, cols]), NT))
            for j in range(tb):
                pr, cols, _ = spots(it, j)
                gv, gk = (sum(x[i][(j - max(0, i - 2)) * QB:(j - max(0, i - 2) + 1) * QB] for i in range(j, j + 3)) for x in (vs, ks))
                dv[cols, pr] = gv.astype(BF)
                dkt[pr, cols] = rope(gk.T, cos_i[:, cols], sin_i[:, cols], -1, head_dim).astype(BF)

        def close_group(g):
            cols = pl.ds(pl.multiple_of(g * CB, CB), CB)
            with jax.named_scope("b_dwqkv"):
                put(spot_of("q", g), dot(hat[:], dqt[cols, :], NT))
                put(spot_of("k", g), dot(hat[:], dkt[cols, :], NT))
                put(spot_of("v", g), dot(hat[:], dv[:, cols]))

        def weights():
            return [pltpu.make_async_copy(s, d, ld.at[10 + i]) for i, (s, d) in enumerate(((wq_h, wq), (wk_h, wk), (wv_h, wv), (x_h, xbuf)))]

        def arrived(p):
            whole = dor.at[pl.ds(aligned(p * pw, pw), pw), :]
            with jax.named_scope("b_hwait"):
                to_left(whole, whole, osnd.at[p], orcv.at[p]).wait()

        def walk(it):
            ahead = it + 1

            @pl.when((lax.rem(ahead, rows) == 0) & (ahead < n_steps))
            def _():
                arrived(ahead // rows)

            @pl.when(it < n_steps)
            def _():
                with jax.named_scope("b_attn"):
                    grads(it - 1)
                    soften(it)
                    score(jnp.minimum(ahead, n_steps - 1))

            @pl.when(it == n_steps)
            def _():
                grads(n_steps - 1)
                for c in weights():
                    c.start()

            p, step = it // rows - 1, lax.rem(it, rows)

            @pl.when((step == 0) & (lax.rem(p, per) == per - 1))
            def _():
                close_group(p // per)

            @pl.when(it == n_steps)
            def _():
                comm.offer(end)

            t = pick(it, tick_after)

            @pl.when(t > 0)
            def _():
                comm.tick(t)

            @pl.when((step == 0) & (p + 3 < n_pairs))
            def _():
                give_out(p + 3)

        for c in lds[:-1]:
            c.wait()
        for i in range(2):
            push_rows(i).wait()
        arrived(0)
        score(0)
        soften(0)
        score(1)
        lds[-1].wait()
        cdiv_loop(n_steps, lambda i: walk(i + 1))
        for c in weights():
            c.wait()

        def into(b):
            r = pl.ds(aligned(b * toks, QB), toks)
            with jax.named_scope("b_into"):
                gnm[r, :] = dot(dqt[:, r], wq[:], TN) + dot(dkt[:, r], wk[:], TN) + dot(dv[r, :], wv[:])

            with jax.named_scope("b_final"):
                for i in range(tb):
                    r = pl.ds(aligned((b * tb + i) * QB, QB), QB)
                    out, dg = norm_back(xbuf[r, :], ga[:], gnm[r, :], gmid[r, :])
                    mbuf[r, :] = out
                    dgain[:8, :] += dg

        def share_gains():
            out_copy.start()
            gains = jnp.concatenate([col_sum(dgain[:8, :]), col_sum(dgain[8:, :]), jnp.zeros((6, width), F32)], axis=0)
            for p in range(n):
                gsend[p, :, :rpd] = gains[:, p * rpd:(p + 1) * rpd]

            def spread(i):
                to = lax.rem(me + i + 1, n)
                pltpu.make_async_remote_copy(src_ref=gsend.at[to], dst_ref=grecv.at[i], send_sem=gsem.at[0], recv_sem=gsem.at[1],
                                             device_id={"seq": to}, device_id_type=MESH).start()

            cdiv_loop(n - 1, spread)

        def finish(i):
            comm.advance(end + i, True)

            @pl.when(i == 1)
            def _():
                cdiv_loop(rows - 2, lambda b: into(b + 1))

            @pl.when(i == LAG + 1)
            def _():
                into(rows - 1)
                share_gains()

        into(0)
        cdiv_loop(4 * LAG - 1, finish)

    score_bufs = [f(3 * QB, 2 * QB) for f in (vf, vm) for _ in range(8)]
    out_copy = pltpu.make_async_copy(mbuf, dx_h, ld.at[0])
    pl.run_scoped(attention, vm(hd, total), vm(hd, rows * ext), vm(rows * ext, hd), vm(rows * ext, hd), vm(hd, rows * WINDOW), vm(total, hd), *score_bufs)
    most, rest = pl.ds(0, end), pl.ds(end, 2)
    keep_most = load(1, fin.at[most], fin_h.at[most])
    to_left(gsend.at[pl.ds(0, n - 1)], grecv, gsem.at[0], gsem.at[1]).wait()
    sums = gsend[me]
    for i in range(n - 1):
        sums = sums + grecv[i]
    fin[end + 1, 0, :8, :128] = sums
    out_copy.wait()
    comm.advance(end + 4 * LAG - 1, True)
    with jax.named_scope("b_end"):
        keep_rest = load(0, fin.at[rest], fin_h.at[rest])
        keep_most.wait()
        keep_rest.wait()


def spread_kernel(dims, dx_i, fin_i, dx_o, dga_o, dgm_o, *refs):
    head_dim, n, width, ff = dims
    outs, (buf, fin), stage, sem = refs[:7], refs[7:9], refs[9:16], refs[16]
    dq, dk, dv, do, dg, du, dd = stage
    nb, nc, sub = ff // CB, width // CB, ff // width
    rpd = width // n
    head, place, end = plan(nb, nc * sub // 2, nc)
    get_fin = pltpu.make_async_copy(fin_i, fin, sem.at[len(outs)])
    get_fin.start()
    cut = buf.shape[0] // nc
    gets, puts = ([pltpu.make_async_copy(s.at[pl.ds(i * cut, cut)], d.at[pl.ds(i * cut, cut)], sem.at[len(outs) + k + i]) for i in range(nc)]
                  for k, s, d in ((1, dx_i, buf), (nc + 1, buf, dx_o)))
    for c in gets:
        c.start()
    get_fin.wait()
    gains = fin[end + 1, 0]
    dga_o[:] = gains[:1, :rpd]
    dgm_o[:] = gains[1:2, :rpd]
    for j in range(nb):
        dg[:, j * CB:(j + 1) * CB] = fin[j, 0]
        du[:, j * CB:(j + 1) * CB] = fin[j, 1]
    for c in range(nc):
        for i in range(sub):
            pair = nb + (c * sub + i) // 2
            dd[i * rpd:(i + 1) * rpd, c * CB:(c + 1) * CB] = fin[pair, i % 2]
    for g in range(nc):
        do[:, g * CB:(g + 1) * CB] = fin[place["o", g]]
        for name, ref in (("q", dq), ("k", dk), ("v", dv)):
            val = fin[place[name, g]]
            for h in range(CB // head_dim):
                ref[g * (CB // head_dim) + h] = val[:, h * head_dim:(h + 1) * head_dim]
    keeps = [pltpu.make_async_copy(s, d, sem.at[i]) for i, (s, d) in enumerate(zip(stage, outs))]
    for c in keeps:
        c.start()
    for get, out in zip(gets, puts):
        get.wait()
        out.start()
    for c in keeps + puts:
        c.wait()


def run_bwd(n, head_dim, ga, gm, x, dout, q, kt, k, v, ha, ot, xm, hm, hmt, qr, lse, cos_t, sin_t, wq, wk, wv, wo, wg, wu, wd, rows):
    total, width = x.shape
    hd, ff = wq.shape[0], wg.shape[1]
    toks = total // rows
    rpd, heads = width // n, hd // head_dim
    nb, nc, sub = ff // CB, width // CB, ff // width
    slots = plan(nb, nc * sub // 2, nc)[2] + 2
    n_pairs = hd // (2 * head_dim)
    f = lambda *s: jax.ShapeDtypeStruct(s, F32)
    dx_t = jax.ShapeDtypeStruct((total, width), BF)
    vm = lambda *s: pltpu.VMEM(s, BF)
    vf = lambda *s: pltpu.VMEM(s, F32)
    dma = lambda *s: pltpu.SemaphoreType.DMA(s)
    line, duo = vf(rows * n_pairs, 8, 2 * QB), (2, SLOTS)
    scratch = [vf(RING, 2, n // 2, 2, rpd, CB), vf(SLOTS, 2, n // 2, rpd, CB), vf(*duo, 2, 2, rpd, CB), vf(*duo, 2, 4, rpd, CB),
               vf(*duo, 2, rpd, CB // 2), vf(*duo, 2, rpd, CB), vf(*duo, 3, rpd, CB), vf(*duo, 4, 4, rpd, CB), vf(*duo, 4, rpd, CB), vf(slots, 2, rpd, CB),
               dma(6, *duo), dma(6, *duo),
               vm(hd, rows * WINDOW), line, line, dma(2), dma(2), dma(n_pairs), dma(n_pairs),
               vf(n, 8, 128), vf(n - 1, 8, 128), dma(2), dma(15),
               vm(total, width), vm(total, width), vf(total, width), vm(total, width), vm(hd, total), vm(width, total), vm(hd, width), vm(hd, total), line, line, vf(*cos_t.shape), vf(*cos_t.shape), vf(*ga.shape), vf(*ga.shape), vf(16, width)]
    mid = pl.pallas_call(
        functools.partial(bwd_kernel, n, head_dim, (rows, toks, width, hd, ff)), out_shape=[dx_t, f(slots, 2, rpd, CB)],
        in_specs=any_spec(24), out_specs=any_spec(2), scratch_shapes=scratch,
        compiler_params=pltpu.CompilerParams(collective_id=1, has_side_effects=True, vmem_limit_bytes=VMEM_LIMIT),
        name="backward")(ga, gm, x, dout, q, kt, k, v, ha, ot, xm, hm, hmt, qr, lse, cos_t, sin_t, wq, wk, wv, wo, wg, wu, wd)
    outs = [f(heads, rpd, head_dim)] * 3 + [f(rpd, width), f(rpd, ff), f(rpd, ff), f(ff // n, width)]
    return pl.pallas_call(
        functools.partial(spread_kernel, (head_dim, n, width, ff)), out_shape=[dx_t, f(1, rpd), f(1, rpd)] + outs,
        in_specs=any_spec(2), out_specs=any_spec(1) + vmem_spec(2) + any_spec(7),
        scratch_shapes=[vm(total, width), vf(slots, 2, rpd, CB), *[vf(*o.shape) for o in outs], dma(8 + 2 * nc)],
        name="spread")(*mid)


def solution(mesh):
    n = mesh.shape["seq"]

    def device_step(hidden, positions, g_attn, g_mlp, w_query, w_key, w_value, w_out, w_gate, w_up, w_down, d_out):
        rows, toks, width = hidden.shape
        layers, _, heads, head_dim = w_query.shape
        hd = heads * head_dim
        half = head_dim // 2
        inv_freq = 1.0 / (10000.0 ** (jnp.arange(half, dtype=F32) * (2.0 / head_dim)))
        turn = lambda w: w[0].transpose(1, 2, 0).reshape(hd, width)
        wq, wk, wv = turn(w_query), turn(w_key), turn(w_value)
        fwd = run_fwd(n, hidden, positions, inv_freq[:, None], g_attn, g_mlp, wq, wk, wv, w_out[0], head_dim)
        out = run_bwd(n, head_dim, g_attn, g_mlp, hidden.reshape(rows * toks, width), d_out.reshape(rows * toks, width), *fwd,
                      wq, wk, wv, w_out[0], w_gate[0], w_up[0], w_down[0], rows)
        dx, dga, dgm, dq, dk, dv, do, dg, du, dd = out
        back = lambda w: w.transpose(1, 0, 2)[None]
        return (dx.reshape(rows, toks, width), dga, dgm, back(dq), back(dk), back(dv), do[None], dg[None], du[None], dd[None])

    tok_spec, grad_spec = P("data", "seq"), P(None, ("data", "seq"))
    in_specs = (tok_spec, tok_spec) + (P(),) * 9 + (tok_spec,)
    out_specs = (tok_spec,) + (grad_spec,) * 9
    return jax.shard_map(device_step, mesh=mesh, in_specs=in_specs, out_specs=out_specs, check_vma=False)
```

profile of v0, /device:TPU:97, one launch (start us, length us, event | category | flops | bytes accessed | tf_op | source)
XLA Modules:
  0.0 171.4 jit_solution(6205632450226390427)
XLA Ops:
  0.6 0.6 negate_power_fusion.invf_h
  1.3 30.0 %forward.1 = (bf16[768,1152]{1,0:T(8,128)(2,1)}, bf16[768,1920]{1,0:T(8,128)(2,1)}, bf16[1920,768]{1,0:T(8,128)(2,1)}, bf16[1920,768]{1,0:T(8,128)(2,1)}, bf16[1...) custom-call(bf16[3,384,768]{2,1,0:T(8,128)(2,1)} %x_h.1, ...), custom_call_target="tpu_custom_call" | custom-call | tf_op jit(solution)/shard_map/forward/pallas_call | solution.py:325
  31.3 136.2 %backward.1 = (bf16[1152,768]{1,0:T(8,128)(2,1)}, f32[27,2,24,256]{3,2,1,0:T(8,128)}) custom-call(f32[1,768]{1,0:T(1,128)} %ga_h.3, f32[1,768]{1,0:T(1,128)} %gm_h.3, bf16[1152,768]{1,0:T(8,128)(2,1)} %bitcast.35, bf16[1152,768]{1,0:T(8,128)(2,1)} %bitcast.47, bf16[768,1152]{1,0:T(8,128)(2,1)} %get-tuple-element.35.q_h, ...), custom_call_target="tpu_custom_call" | custom-call | tf_op jit(solution)/shard_map/backward/pallas_call | solution.py:943
  167.5 3.7 %spread.1 = (bf16[1152,768]{1,0:T(8,128)(2,1)}, f32[1,24]{1,0:T(1,128)}, f32[1,24]{1,0:T(1,128)}, f32[12,24,64]{2,1,0:T(8,128)}, f32[12,24,64]{2,1,0:T(8,128)}, ...) custom-call(bf16[1152,768]{1,0:T(8,128)(2,1)} %get-tuple-element.48., ...), custom_call_target="tpu_custom_call" | custom-call | tf_op jit(solution)/shard_map/spread/pallas_call | solution.py:949
where the time goes:
time: 172 us; the launch traced here: 171 us
  Pallas kernels  170 us (99%)
    pallas_call x1, Pallas kernels, run_bwd(): pl.pallas_call(functools.partial(bwd_kernel, n, head_dim, (rows, toks, wi...  136 us
    pallas_call x1, Pallas kernels, run_fwd(): pl.pallas_call(functools.partial(fwd_kernel, n, head_dim), out_shape=outs...  30 us
    pallas_call x1, Pallas kernels, run_bwd(): pl.pallas_call(functools.partial(spread_kernel, (head_dim, n, width, ff))...  3.72 us

commit v1 on v0

--- a/solution.py
+++ b/solution.py
@@ -167,7 +167,9 @@
         acc[:] = dot(wq[:], hb[:], NT)
         acc2[:] = dot(wk[:], hb[:], NT)
         put_q(acc)
+        send_pos.wait()
         acc[:] = dot(wv[:], hb[:], NT)
+        angles(cos_h, sin_h, pos_halo[:, toks - WINDOW:])
         put_own(acc2, kt, k)
         put_own(acc, vt, v)
     keep_q = pltpu.make_async_copy(q, q_h, st.at[1])
@@ -179,8 +181,6 @@
 
     for b in range(rows):
         push_q(b).start()
-    send_pos.wait()
-    angles(cos_h, sin_h, pos_halo[:, toks - WINDOW:])
 
     def keeps(b):
         wide, cols = pl.ds(pl.multiple_of(b * ext, QB), ext), pl.ds(pl.multiple_of(b * toks, QB), toks)
@@ -961,10 +961,10 @@
         layers, _, heads, head_dim = w_query.shape
         hd = heads * head_dim
         half = head_dim // 2
-        inv_freq = 1.0 / (10000.0 ** (jnp.arange(half, dtype=F32) * (2.0 / head_dim)))
+        inv_freq = 1.0 / (np.float32(10000.0) ** (np.arange(half, dtype=np.float32) * np.float32(2.0 / head_dim)))
         turn = lambda w: w[0].transpose(1, 2, 0).reshape(hd, width)
         wq, wk, wv = turn(w_query), turn(w_key), turn(w_value)
-        fwd = run_fwd(n, hidden, positions, inv_freq[:, None], g_attn, g_mlp, wq, wk, wv, w_out[0], head_dim)
+        fwd = run_fwd(n, hidden, positions, jnp.asarray(inv_freq.astype(np.float32)[:, None]), g_attn, g_mlp, wq, wk, wv, w_out[0], head_dim)
         out = run_bwd(n, head_dim, g_attn, g_mlp, hidden.reshape(rows * toks, width), d_out.reshape(rows * toks, width), *fwd,
                       wq, wk, wv, w_out[0], w_gate[0], w_up[0], w_down[0], rows)
         dx, dga, dgm, dq, dk, dv, do, dg, du, dd = out

time: 172 us -> 171 us (level)
    pallas_call x1, Pallas kernels: 30 us -> 32.3 us  [run_fwd(): pl.pallas_call(functools.partial(fwd_kernel, n, head_dim), out_shape=outs...]
    pallas_call x1, Pallas kernels: 136 us -> 134 us  [run_bwd(): pl.pallas_call(functools.partial(bwd_kernel, n, head_dim, (rows, toks, wi...]
where the time goes in v1:
time: 171 us
  Pallas kernels  170 us (99%)
    pallas_call x1, Pallas kernels, run_bwd(): pl.pallas_call(functools.partial(bwd_kernel, n, head_dim, (rows, toks, wi...  134 us
    pallas_call x1, Pallas kernels, run_fwd(): pl.pallas_call(functools.partial(fwd_kernel, n, head_dim), out_shape=outs...  32.3 us
    pallas_call x1, Pallas kernels, run_bwd(): pl.pallas_call(functools.partial(spread_kernel, (head_dim, n, width, ff))...  3.72 us

profile of v1, /device:TPU:97, one launch (start us, length us, event | category | flops | bytes accessed | tf_op | source)
XLA Modules:
  0.0 171.0 jit_solution(6809897810125445064)
XLA Ops:
  0.6 32.3 %forward.1 = (bf16[768,1152]{1,0:T(8,128)(2,1)}, bf16[768,1920]{1,0:T(8,128)(2,1)}, bf16[1920,768]{1,0:T(8,128)(2,1)}, bf16[1920,768]{1,0:T(8,128)(2,1)}, bf16[1...) custom-call(bf16[3,384,768]{2,1,0:T(8,128)(2,1)} %x_h.1, ...), custom_call_target="tpu_custom_call" | custom-call | tf_op jit(solution)/shard_map/forward/pallas_call | solution.py:325
  33.0 134.2 %backward.1 = (bf16[1152,768]{1,0:T(8,128)(2,1)}, f32[27,2,24,256]{3,2,1,0:T(8,128)}) custom-call(f32[1,768]{1,0:T(1,128)} %ga_h.3, f32[1,768]{1,0:T(1,128)} %gm_h.3, bf16[1152,768]{1,0:T(8,128)(2,1)} %bitcast.35, bf16[1152,768]{1,0:T(8,128)(2,1)} %bitcast.47, bf16[768,1152]{1,0:T(8,128)(2,1)} %get-tuple-element.35.q_h, ...), custom_call_target="tpu_custom_call" | custom-call | tf_op jit(solution)/shard_map/backward/pallas_call | solution.py:943
  167.1 3.7 %spread.1 = (bf16[1152,768]{1,0:T(8,128)(2,1)}, f32[1,24]{1,0:T(1,128)}, f32[1,24]{1,0:T(1,128)}, f32[12,24,64]{2,1,0:T(8,128)}, f32[12,24,64]{2,1,0:T(8,128)}, ...) custom-call(bf16[1152,768]{1,0:T(8,128)(2,1)} %get-tuple-element.48., ...), custom_call_target="tpu_custom_call" | custom-call | tf_op jit(solution)/shard_map/spread/pallas_call | solution.py:949

commit v2 on v1

--- a/solution.py
+++ b/solution.py
@@ -695,8 +695,7 @@
             cdiv_loop(nc, out_grad)
         first_tick = nb + nc + 1
         comm.tick(first_tick - 1)
-        ends = [rows * p for p in range(1, n_pairs + 1)]
-        steps = sorted([1, ends[1] - 1, ends[-2] - 1, ends[-1] - 1, *ends[1:]])
+        steps = [1, 4, 6, 8, 10, 13, 15, 17, 18]
         tick_after = {s: first_tick + i for i, s in enumerate(steps)}
         assert first_tick + len(steps) == end
         upper = upper_mask()

time: 171 us -> 171 us (level)
  no operation moved by 1% of the time
where the time goes in v2:
time: 171 us
  Pallas kernels  170 us (99%)
    pallas_call x1, Pallas kernels, run_bwd(): pl.pallas_call(functools.partial(bwd_kernel, n, head_dim, (rows, toks, wi...  134 us
    pallas_call x1, Pallas kernels, run_fwd(): pl.pallas_call(functools.partial(fwd_kernel, n, head_dim), out_shape=outs...  32.3 us
    pallas_call x1, Pallas kernels, run_bwd(): pl.pallas_call(functools.partial(spread_kernel, (head_dim, n, width, ff))...  3.72 us

profile of v2, /device:TPU:97, one launch (start us, length us, event | category | flops | bytes accessed | tf_op | source)
XLA Modules:
  0.0 170.5 jit_solution(4994662393664830227)
XLA Ops:
  0.6 32.3 %forward.1 = (bf16[768,1152]{1,0:T(8,128)(2,1)}, bf16[768,1920]{1,0:T(8,128)(2,1)}, bf16[1920,768]{1,0:T(8,128)(2,1)}, bf16[1920,768]{1,0:T(8,128)(2,1)}, bf16[1...) custom-call(bf16[3,384,768]{2,1,0:T(8,128)(2,1)} %x_h.1, ...), custom_call_target="tpu_custom_call" | custom-call | tf_op jit(solution)/shard_map/forward/pallas_call | solution.py:325
  33.0 133.7 %backward.1 = (bf16[1152,768]{1,0:T(8,128)(2,1)}, f32[27,2,24,256]{3,2,1,0:T(8,128)}) custom-call(f32[1,768]{1,0:T(1,128)} %ga_h.3, f32[1,768]{1,0:T(1,128)} %gm_h.3, bf16[1152,768]{1,0:T(8,128)(2,1)} %bitcast.35, bf16[1152,768]{1,0:T(8,128)(2,1)} %bitcast.47, bf16[768,1152]{1,0:T(8,128)(2,1)} %get-tuple-element.35.q_h, ...), custom_call_target="tpu_custom_call" | custom-call | tf_op jit(solution)/shard_map/backward/pallas_call | solution.py:942
  166.6 3.7 %spread.1 = (bf16[1152,768]{1,0:T(8,128)(2,1)}, f32[1,24]{1,0:T(1,128)}, f32[1,24]{1,0:T(1,128)}, f32[12,24,64]{2,1,0:T(8,128)}, f32[12,24,64]{2,1,0:T(8,128)}, ...) custom-call(bf16[1152,768]{1,0:T(8,128)(2,1)} %get-tuple-element.48., ...), custom_call_target="tpu_custom_call" | custom-call | tf_op jit(solution)/shard_map/spread/pallas_call | solution.py:948
